TPU v7x, 16 devices: a 4x2x1 block of a 4x4x8 slice. The times are simulated.
16 devices in a mesh: rep: 2 (over y, z), dp: 8 (over x, core).
Axes of the slice: x: 4, y: 2, z: 1, core: 2. Of those that a mesh axis runs over, the one named last changes fastest.
The devices are a block of a 4x4x8 slice.
Arguments:
- x: bfloat16 [16, 2048, 1024], P(('rep', 'dp')), parts along dimension 0
- dy: bfloat16 [16, 2048, 1024], P(('rep', 'dp')), parts along dimension 0
- w_gate: bfloat16 [2, 1024, 2816], P(None, 'dp')
- w_up: bfloat16 [2, 1024, 2816], P(None, 'dp')
- w_down: bfloat16 [2, 2816, 1024], P(None, 'dp')
- m_w_gate: float32 [2, 1024, 2816], P(None, 'dp')
- m_w_up: float32 [2, 1024, 2816], P(None, 'dp')
- m_w_down: float32 [2, 2816, 1024], P(None, 'dp')
- v_w_gate: float32 [2, 1024, 2816], P(None, 'dp')
- v_w_up: float32 [2, 1024, 2816], P(None, 'dp')
- v_w_down: float32 [2, 2816, 1024], P(None, 'dp')
Outputs:
- output 1: bfloat16 [4, 1024, 2816], P('rep', 'dp'), parts along dimension 0
- output 2: bfloat16 [4, 1024, 2816], P('rep', 'dp'), parts along dimension 0
- output 3: bfloat16 [4, 2816, 1024], P('rep', 'dp'), parts along dimension 0
- output 4: float32 [4, 1024, 2816], P('rep', 'dp'), parts along dimension 0
- output 5: float32 [4, 1024, 2816], P('rep', 'dp'), parts along dimension 0
- output 6: float32 [4, 2816, 1024], P('rep', 'dp'), parts along dimension 0
- output 7: float32 [4, 1024, 2816], P('rep', 'dp'), parts along dimension 0
- output 8: float32 [4, 1024, 2816], P('rep', 'dp'), parts along dimension 0
- output 9: float32 [4, 2816, 1024], P('rep', 'dp'), parts along dimension 0
There are 2 independent parts. A program takes and returns all parts, laid end to end along the dimension named above; an argument that names none is the same for every part.
All inputs are finite; a program needn't handle non-finite values.
Results may differ from a plain program's by a relative error of at most 0.022.
Values are sent between devices in bfloat16 or wider.
A program may use at most 768 MiB of HBM per device.

v0:
```python
import jax
import jax.numpy as jnp
from jax import lax
from jax.sharding import PartitionSpec as P

NAMES = ("w_gate", "w_up", "w_down")


def matmul(a, w):
    return jnp.dot(a, w, preferred_element_type=jnp.float32).astype(jnp.bfloat16)


def normed(h):
    wide = h.astype(jnp.float32)
    scale = lax.rsqrt(jnp.mean(wide**2, -1, keepdims=True) + 1e-6)
    return (wide * scale).astype(jnp.bfloat16)


def layer(h, w):
    a = normed(h)
    gate = jnp.dot(a, w["w_gate"], preferred_element_type=jnp.float32)
    up = jnp.dot(a, w["w_up"], preferred_element_type=jnp.float32)
    return h + matmul((jax.nn.silu(gate) * up).astype(jnp.bfloat16), w["w_down"])


def adamw(w, m, v, g):
    m = 0.9 * m + 0.1 * g
    v = 0.95 * v + 0.05 * g * g
    step = m * lax.rsqrt(v + 1e-8) + 0.1 * w
    return (w - 0.02 * step).astype(jnp.bfloat16), m, v


def clipped(gradients, sum_of_squares, count):
    factor = jnp.minimum(1.0, 0.5 * lax.rsqrt(sum_of_squares / count + 1e-30))
    return [g * factor for g in gradients]


def solution(mesh):
    def fetched(weights, number):
        return {name: lax.all_gather(w[number], "dp", axis=0, tiled=True) for name, w in zip(NAMES, weights, strict=True)}

    def step(x, dy, *arrays):
        weights, m, v = (arrays[i : i + 3] for i in (0, 3, 6))
        layers = weights[0].shape[0]
        h, kept = x[0], []
        for number in range(layers):
            kept.append(h)
            h = layer(h, fetched(weights, number))
        by_h, mine = dy[0], [None] * layers
        for number in reversed(range(layers)):
            _, back = jax.vjp(lambda w, h: layer(h, w), fetched(weights, number), kept[number])
            by_w, by_h = back(by_h)
            mine[number] = [lax.psum_scatter(by_w[name], "dp", scatter_dimension=0, tiled=True) for name in NAMES]
        gradients = [jnp.stack([mine[number][i] for number in range(layers)]).astype(jnp.float32) for i in range(3)]
        squares = lax.psum(sum(jnp.sum(g * g) for g in gradients), "dp")
        gradients = clipped(gradients, squares, lax.psum(1, "dp") * sum(g.size for g in gradients))
        new = [adamw(w.astype(jnp.float32), m, v, g) for w, m, v, g in zip(weights, m, v, gradients, strict=True)]
        return tuple(one[which] for which in range(3) for one in new)

    states, cut = P(("rep", "dp"), None, None), P(None, "dp", None)
    return jax.shard_map(
        step,
        mesh=mesh,
        in_specs=(states, states) + (cut,) * 9,
        out_specs=(P("rep", "dp", None),) * 9,
        check_vma=False,
    )
```

profile of v0, /device:TPU:113, one launch (start us, length us, event | category | flops | bytes accessed | tf_op | source)
XLA Modules:
  0.0 602.1 jit_solution(2238377583476725769)
XLA Ops:
  7.2 0.1 all-gather.13.cloned.1.call-start
  7.3 2.6 fusion.94
  9.9 0.1 all-gather.13.cloned.1.call-update
  9.9 0.1 all-gather.15.cloned.1.call-start
  10.0 2.5 fusion.93
  12.5 0.1 all-gather.15.cloned.1.call-update
  12.6 0.1 all-gather.17.cloned.1.call-start
  12.7 1.2 fusion.92
  13.9 0.1 all-gather.17.cloned.1.call-update
  13.9 0.1 all-gather.21.cloned.1.call-start
  14.0 0.6 all-gather.21.cloned.1.call-update
  14.6 0.1 all-gather.23.cloned.1.call-start
  14.7 0.6 all-gather.23.cloned.1.call-update
  15.2 0.1 all-gather.19.cloned.1.call-start
  15.3 0.6 all-gather.19.cloned.1.call-update
  15.9 0.1 reduce-scatter.15.cloned.1.call-start
  15.9 6.5 %copy.20 = bf16[1,2048,1024]{1,2,0:T(8,128)(2,1)} copy(bf16[1,2048,1024]{2,1,0:T(8,128)(2,1)} %param.11) | data formatting | bytes 8388608 | tf_op args[0]
  22.5 3.1 fusion.15
  25.6 6.6 %copy.21 = bf16[1,2048,1024]{1,2,0:T(8,128)(2,1)} copy(bf16[1,2048,1024]{2,1,0:T(8,128)(2,1)} %param.12) | data formatting | bytes 8388608 | tf_op args[1]
  32.1 15.7 %all-gather.13.cloned.1.call-done = bf16[1,1024,2816]{2,1,0:T(8,128)(2,1)} async-done(((bf16[1,128,2816]{2,1,0:T(8,128)(2,1)}), bf16[1,1024,2816]{2,1,0:T(8,128)(2,1)}) %all-gather.13.cloned.1.call-update) | async-done | bytes 5767184 | tf_op jit(solution)/shard_map/all_gather | solution.py:40
  47.8 20.0 %fusion.35 = f32[2048,2816]{1,0:T(8,128)} fusion(bf16[1,1024,2816]{2,1,0:T(8,128)(2,1)} %all-gather.13.cloned.1.call-done, bf16[1,2048,1024]{1,2,0:T(8,128)(2,1)} %copy.20, f32[2048]{0:T(1024)S(1)} %add_rsqrt_fusion), kind=kOutput, calls=%fused_computation.53 | convolution fusion | flops 11817451520 | bytes 33038336 | tf_op jit(solution)/shard_map/dot_general | solution.py:21
  67.8 16.6 %all-gather.15.cloned.1.call-done = bf16[1,1024,2816]{2,1,0:T(8,128)(2,1)} async-done(((bf16[1,128,2816]{2,1,0:T(8,128)(2,1)}), bf16[1,1024,2816]{2,1,0:T(8,128)(2,1)}) %all-gather.15.cloned.1.call-update) | async-done | bytes 5767184 | tf_op jit(solution)/shard_map/all_gather | solution.py:40
  84.4 27.8 %multiply_convert_fusion.1 = (bf16[2048,2816]{1,0:T(8,128)(2,1)}, f32[2048,2816]{1,0:T(8,128)}) fusion(f32[2048,2816]{1,0:T(8,128)} %fusion.35, bf16[1,1024,2816]{2,1,0:T(8,128)(2,1)} %all-gather.15.cloned.1.call-done, bf16[1,2048,1024]{1,2,0:T(8,128)(2,1)} %copy.20, f32[2048]{0:T(1024)S(1)} %add_rsqrt_fusion), kind=kOutput, calls=%fused_computation.17 | convolution fusion | flops 11852054528 | bytes 67641344 | tf_op jit(solution)/shard_map/dot_general | solution.py:22
  112.2 8.8 %all-gather.17.cloned.1.call-done = bf16[1,2816,1024]{2,1,0:T(8,128)(2,1)} async-done(((bf16[1,352,1024]{2,1,0:T(8,128)(2,1)}), bf16[1,2816,1024]{2,1,0:T(8,128)(2,1)}) %all-gather.17.cloned.1.call-update) | async-done | bytes 5767184 | tf_op jit(solution)/shard_map/all_gather | solution.py:40
  121.0 19.8 %fusion.19 = (f32[2048]{0:T(1024)S(1)}, bf16[2048,1024]{0,1:T(8,128)(2,1)}) fusion(bf16[2048,2816]{1,0:T(8,128)(2,1)} %get-tuple-element.24, bf16[1,2816,1024]{2,1,0:T(8,128)(2,1)} %all-gather.17.cloned.1.call-done, bf16[1,2048,1024]{1,2,0:T(8,128)(2,1)} %copy.20), kind=kOutput, calls=%fused_computation.37 | convolution fusion | flops 11821643776 | bytes 25698304 | tf_op jit(solution)/shard_map/dot_general | solution.py:10
  140.8 16.6 %all-gather.21.cloned.1.call-done = bf16[1,2816,1024]{2,1,0:T(8,128)(2,1)} async-done(((bf16[1,352,1024]{2,1,0:T(8,128)(2,1)}), bf16[1,2816,1024]{2,1,0:T(8,128)(2,1)}) %all-gather.21.cloned.1.call-update) | async-done | bytes 5767184 | tf_op jit(solution)/shard_map/all_gather | solution.py:40
  157.4 18.1 %convolution_convert_fusion.1 = bf16[2048,2816]{1,0:T(8,128)(2,1)} fusion(bf16[1,2816,1024]{2,1,0:T(8,128)(2,1)} %all-gather.21.cloned.1.call-done, bf16[1,2048,1024]{2,1,0:T(8,128)(2,1)} %param.12), kind=kOutput, calls=%fused_computation.29 | convolution fusion | flops 11816927232 | bytes 21495808 | tf_op jit(solution)/shard_map/transpose(jvp())/dot_general | solution.py:10
  175.6 18.3 %all-gather.23.cloned.1.call-done = bf16[1,1024,2816]{2,1,0:T(8,128)(2,1)} async-done(((bf16[1,128,2816]{2,1,0:T(8,128)(2,1)}), bf16[1,1024,2816]{2,1,0:T(8,128)(2,1)}) %all-gather.23.cloned.1.call-update) | async-done | bytes 5767184 | tf_op jit(solution)/shard_map/all_gather | solution.py:40
  193.9 20.1 %fusion.22 = f32[2048,2816]{1,0:T(8,128)} fusion(bf16[1,1024,2816]{2,1,0:T(8,128)(2,1)} %all-gather.23.cloned.1.call-done, bf16[2048,1024]{0,1:T(8,128)(2,1)} %get-tuple-element.27, f32[2048]{0:T(1024)S(1)} %fusion.80), kind=kOutput, calls=%fused_computation.40 | convolution fusion | flops 11817451520 | bytes 33038336 | tf_op jit(solution)/shard_map/jvp()/dot_general | solution.py:22
  213.9 16.4 %all-gather.19.cloned.1.call-done = bf16[1,1024,2816]{2,1,0:T(8,128)(2,1)} async-done(((bf16[1,128,2816]{2,1,0:T(8,128)(2,1)}), bf16[1,1024,2816]{2,1,0:T(8,128)(2,1)}) %all-gather.19.cloned.1.call-update) | async-done | bytes 5767184 | tf_op jit(solution)/shard_map/all_gather | solution.py:40
  230.3 34.4 %fusion.2 = (bf16[2048,2816]{1,0:T(8,128)(2,1)}, f32[2048,2816]{1,0:T(8,128)}) fusion(f32[2048,2816]{1,0:T(8,128)} %fusion.22, bf16[2048,2816]{1,0:T(8,128)(2,1)} %convolution_convert_fusion.1, bf16[1,1024,2816]{2,1,0:T(8,128)(2,1)} %all-gather.19.cloned.1.call-done, bf16[2048,1024]{0,1:T(8,128)(2,1)} %get-tuple-element.27, f32[2048]{0:T(1024)S(1)} %fusion.80), kind=kOutput, calls=%fused_computation.8 | convolution fusion | flops 11886657536 | bytes 79175680 | tf_op jit(solution)/shard_map/jvp()/dot_general | solution.py:21
  264.7 21.7 %fusion.12 = bf16[2048,1024]{0,1:T(8,128)(2,1)} fusion(bf16[2048,2816]{1,0:T(8,128)(2,1)} %convolution_convert_fusion.1, bf16[1,1024,2816]{2,1,0:T(8,128)(2,1)} %all-gather.23.cloned.1.call-done, f32[2048,2816]{1,0:T(8,128)} %get-tuple-element.29), kind=kOutput, calls=%fused_computation.21 | convolution fusion | flops 11845763072 | bytes 44564480 | tf_op jit(solution)/shard_map/transpose(jvp())/dot_general | solution.py:22
  286.4 18.9 %fusion.21 = (f32[2048]{0:T(1024)S(1)}, bf16[2048,1024]{0,1:T(8,128)(2,1)S(1)}) fusion(bf16[2048,1024]{0,1:T(8,128)(2,1)} %get-tuple-element.27, bf16[2048,1024]{0,1:T(8,128)(2,1)} %fusion.12, bf16[2048,2816]{1,0:T(8,128)(2,1)} %get-tuple-element.28, bf16[1,1024,2816]{2,1,0:T(8,128)(2,1)} %all-gather.19.cloned.1.call-done), kind=kOutput, calls=%fused_computation.39 | convolution fusion | flops 11821643776 | bytes 29892608 | tf_op jit(solution)/shard_map/transpose(jvp())/dot_general | solution.py:21
  305.4 3.6 fusion.43
  309.0 2.0 copy-done.6
  311.0 17.1 %convolution_convert_fusion.2 = bf16[2816,1024]{1,0:T(8,128)(2,1)} fusion(bf16[2048,2816]{1,0:T(8,128)(2,1)} %get-tuple-element.24, bf16[2048,1024]{0,1:T(8,128)(2,1)S(1)} %fusion.43), kind=kOutput, calls=%fused_computation.59 | convolution fusion | flops 11814043648 | bytes 21495808 | tf_op jit(solution)/shard_map/transpose(jvp())/dot_general | solution.py:10
  328.1 0.1 reduce-scatter.15.cloned.1.call-update
  328.2 0.1 reduce-scatter.17.cloned.1.call-start
  328.3 23.5 %fusion.37 = bf16[2816,1024]{1,0:T(8,128)(2,1)} fusion(f32[2048,2816]{1,0:T(8,128)} %fusion.22, bf16[1,2048,1024]{2,1,0:T(8,128)(2,1)} %param.12, f32[2048,2816]{1,0:T(8,128)} %get-tuple-element.29), kind=kOutput, calls=%fused_computation.55 | convolution fusion | flops 11848646656 | bytes 56098816 | tf_op jit(solution)/shard_map/transpose(jvp())/dot_general | solution.py:10
  351.8 0.1 reduce-scatter.17.cloned.1.call-update
  351.8 0.1 reduce-scatter.11.cloned.1.call-start
  351.9 18.5 %convolution_convert_fusion = bf16[2048,2816]{1,0:T(8,128)(2,1)} fusion(bf16[2048,1024]{0,1:T(8,128)(2,1)} %copy-done.6, bf16[1,2816,1024]{2,1,0:T(8,128)(2,1)} %all-gather.17.cloned.1.call-done), kind=kOutput, calls=%fused_computation.28 | convolution fusion | flops 11816927232 | bytes 21495808 | tf_op jit(solution)/shard_map/transpose(jvp())/dot_general | solution.py:10
  370.4 22.4 %fusion.42 = bf16[1024,2816]{1,0:T(8,128)(2,1)} fusion(bf16[2048,2816]{1,0:T(8,128)(2,1)} %convolution_convert_fusion, f32[2048,2816]{1,0:T(8,128)} %fusion.35, bf16[1,2048,1024]{1,2,0:T(8,128)(2,1)} %copy.20, f32[2048]{0:T(1024)S(1)} %copy-done.20), kind=kOutput, calls=%fused_computation.58 | convolution fusion | flops 11854938112 | bytes 44572672 | tf_op jit(solution)/shard_map/transpose(jvp())/dot_general | solution.py:22
  392.9 0.1 reduce-scatter.13.cloned.1.call-start
  393.0 0.6 copy-done.16
  393.5 22.6 %fusion.38 = bf16[1024,2816]{1,0:T(8,128)(2,1)} fusion(bf16[2048,2816]{1,0:T(8,128)(2,1)} %convolution_convert_fusion.1, bf16[2048,1024]{0,1:T(8,128)(2,1)} %get-tuple-element.27, f32[2048]{0:T(1024)S(1)} %copy-done.16, f32[2048,2816]{1,0:T(8,128)} %get-tuple-element.29), kind=kOutput, calls=%fused_computation.56 | convolution fusion | flops 11854938112 | bytes 44572672 | tf_op jit(solution)/shard_map/transpose(jvp())/dot_general | solution.py:22
  416.2 0.1 reduce-scatter.7.cloned.1.call-start
  416.2 26.9 %fusion.39 = bf16[1024,2816]{1,0:T(8,128)(2,1)} fusion(f32[2048,2816]{1,0:T(8,128)} %fusion.35, f32[2048,2816]{1,0:T(8,128)} %get-tuple-element.25, bf16[2048,2816]{1,0:T(8,128)(2,1)} %convolution_convert_fusion, bf16[1,2048,1024]{1,2,0:T(8,128)(2,1)} %copy.20, f32[2048]{0:T(1024)S(1)} %copy-done.20), kind=kOutput, calls=%fused_computation.57 | convolution fusion | flops 11883773952 | bytes 67641344 | tf_op jit(solution)/shard_map/transpose(jvp())/dot_general | solution.py:21
  443.2 0.1 reduce-scatter.9.cloned.1.call-start
  443.3 18.8 %convolution_convert_fusion.3 = bf16[1024,2816]{1,0:T(8,128)(2,1)} fusion(bf16[2048,2816]{1,0:T(8,128)(2,1)} %get-tuple-element.28, bf16[2048,1024]{0,1:T(8,128)(2,1)} %get-tuple-element.27, f32[2048]{0:T(1024)S(1)} %copy-done.16), kind=kOutput, calls=%fused_computation.60 | convolution fusion | flops 11817451520 | bytes 21504000 | tf_op jit(solution)/shard_map/transpose(jvp())/dot_general | solution.py:21
  462.2 2.8 fusion.62
  465.0 15.2 %reduce-scatter.13.cloned.1.call-done = bf16[128,2816]{1,0:T(8,128)(2,1)} async-done(((bf16[1024,2816]{1,0:T(8,128)(2,1)}), bf16[128,2816]{1,0:T(8,128)(2,1)}) %reduce-scatter.13.cloned.1.call-update) | async-done | bytes 720912 | tf_op jit(solution)/shard_map/reduce_scatter | solution.py:53
  480.2 2.7 fusion.61
  482.9 36.3 %reduce-scatter.7.cloned.1.call-done = bf16[128,2816]{1,0:T(8,128)(2,1)} async-done(((bf16[1024,2816]{1,0:T(8,128)(2,1)}), bf16[128,2816]{1,0:T(8,128)(2,1)}) %reduce-scatter.7.cloned.1.call-update) | async-done | bytes 720912 | tf_op jit(solution)/shard_map/reduce_scatter | solution.py:53
  519.2 38.8 %reduce-scatter.9.cloned.1.call-done = bf16[128,2816]{1,0:T(8,128)(2,1)} async-done(((bf16[1024,2816]{1,0:T(8,128)(2,1)}), bf16[128,2816]{1,0:T(8,128)(2,1)}) %reduce-scatter.9.cloned.1.call-update) | async-done | bytes 720912 | tf_op jit(solution)/shard_map/reduce_scatter | solution.py:53
  558.0 2.8 fusion.60
  562.7 14.5 %psum.7 = f32[]{:T(128)} all-reduce(f32[]{:T(128)S(6)} %add.99), channel_id=1, replica_groups=mesh['rep'=2,'dp'=8] {'dp'}, use_global_device_ids=true, to_apply=%region_12.13 | all-reduce | flops 1 | bytes 8 | tf_op jit(solution)/shard_map/psum | solution.py:55
  578.0 6.6 %fusion.68 = (bf16[2,352,1024]{2,1,0:T(8,128)(2,1)}, f32[2,352,1024]{2,1,0:T(8,128)}, f32[2,352,1024]{2,1,0:T(8,128)}) fusion(bf16[2,352,1024]{2,1,0:T(8,128)(2,1)S(1)} %copy-done.4, f32[]{:T(128)S(6)} %min_shard_map.3, bf16[1,352,1024]{2,1,0:T(8,128)(2,1)} %bitcast.69, bf16[1,352,1024]{2,1,0:T(8,128)(2,1)} %bitcast.67, f32[2,352,1024]{2,1,0:T(8,128)} %param.21, ...), kind=kLoop, calls=%fused_computation.98 | loop fusion | flops 14417920 | bytes 15859716 | tf_op jit(solution)/shard_map/convert_element_type | solution.py:30
  584.6 1.4 copy-done.8
  586.1 0.8 copy-done.9
  586.9 0.8 copy-done.10
  587.7 0.1 copy-done.11
  587.8 0.2 copy-done.12
  588.0 6.8 %fusion.59 = (bf16[2,128,2816]{2,1,0:T(8,128)(2,1)}, f32[2,128,2816]{2,1,0:T(8,128)}, f32[2,128,2816]{2,1,0:T(8,128)}, bf16[2,128,2816]{2,1,0:T(8,128)(2,1)}, f3...) fusion(bf16[2,128,2816]{2,1,0:T(8,128)(2,1)S(1)} %copy-done.1, f32[]{:T(128)S(6)} %min_shard_map.3, ...), kind=kLoop, calls=%fused_computation.89 | loop fusion | flops 28835840 | bytes 31719428 | tf_op jit(solution)/shard_map/convert_element_type | solution.py:30
  (45 shorter events, 0.4 us)
Async XLA Ops:
  7.2 5.5 copy-start.3
  7.2 40.6 %all-gather.13.cloned.1.call-start = ((), (), s32[]{:S(2)}) async-start(), calls=%async_computation.12 | async-start | bytes 6488064 | tf_op jit(solution)/shard_map/all_gather | solution.py:40
  9.9 74.5 %all-gather.15.cloned.1.call-start = ((), (), s32[]{:S(2)}) async-start(), calls=%async_computation.13 | async-start | bytes 6488064 | tf_op jit(solution)/shard_map/all_gather | solution.py:40
  12.6 108.4 %all-gather.17.cloned.1.call-start = ((), (), s32[]{:S(2)}) async-start(), calls=%async_computation.14 | async-start | bytes 6488064 | tf_op jit(solution)/shard_map/all_gather | solution.py:40
  13.9 143.5 %all-gather.21.cloned.1.call-start = ((), (), s32[]{:S(2)}) async-start(), calls=%async_computation.16 | async-start | bytes 6488064 | tf_op jit(solution)/shard_map/all_gather | solution.py:40
  14.6 179.3 %all-gather.23.cloned.1.call-start = ((), (), s32[]{:S(2)}) async-start(), calls=%async_computation.17 | async-start | bytes 6488064 | tf_op jit(solution)/shard_map/all_gather | solution.py:40
  15.2 215.1 %all-gather.19.cloned.1.call-start = ((), (), s32[]{:S(2)}) async-start(), calls=%async_computation.15 | async-start | bytes 6488064 | tf_op jit(solution)/shard_map/all_gather | solution.py:40
  15.9 446.3 %reduce-scatter.15.cloned.1.call-start = ((), (), s32[]{:S(2)}) async-start(), calls=%async_computation.10 | async-start | bytes 6488064 | tf_op jit(solution)/shard_map/reduce_scatter | solution.py:53
  25.5 58.9 %copy-start.19 = (f32[2048]{0:T(1024)}, f32[2048]{0:T(1024)S(1)}, u32[]{:S(2)}) copy-start(f32[2048]{0:T(1024)S(1)} %add_rsqrt_fusion) | copy-start | bytes 24580
  140.8 34.8 %copy-start.17 = (f32[2048]{0:T(1024)}, f32[2048]{0:T(1024)S(1)}, u32[]{:S(2)}) copy-start(f32[2048]{0:T(1024)S(1)} %get-tuple-element.26) | copy-start | bytes 24580
  140.8 164.6 %copy-start.15 = (f32[2048]{0:T(1024)}, f32[2048]{0:T(1024)S(1)}, u32[]{:S(2)}) copy-start(f32[2048]{0:T(1024)S(1)} %fusion.80) | copy-start | bytes 24580
  286.4 18.9 %copy-start.18 = (f32[2048]{0:T(1024)S(1)}, f32[2048]{0:T(1024)}, u32[]{:S(2)}) copy-start(f32[2048]{0:T(1024)} %copy-done.17) | copy-start | bytes 24580
  286.4 18.9 %copy-start = (bf16[1,2048,1024]{1,2,0:T(8,128)(2,1)S(1)}, bf16[1,2048,1024]{1,2,0:T(8,128)(2,1)}, u32[]{:S(2)}) copy-start(bf16[1,2048,1024]{1,2,0:T(8,128)(2,1)} %copy.21) | copy-start | bytes 12582916
  286.4 18.9 %copy-start.5 = (bf16[2048,1024]{0,1:T(8,128)(2,1)S(1)}, bf16[2048,1024]{0,1:T(8,128)(2,1)}, u32[]{:S(2)}) copy-start(bf16[2048,1024]{0,1:T(8,128)(2,1)} %get-tuple-element.27) | copy-start | bytes 12582916
  309.0 2.0 copy-start.6
  328.2 134.0 %reduce-scatter.17.cloned.1.call-start = ((), (), s32[]{:S(2)}) async-start(), calls=%async_computation.11 | async-start | bytes 6488064 | tf_op jit(solution)/shard_map/reduce_scatter | solution.py:53
  351.8 18.6 %copy-start.20 = (f32[2048]{0:T(1024)S(1)}, f32[2048]{0:T(1024)}, u32[]{:S(2)}) copy-start(f32[2048]{0:T(1024)} %copy-done.19) | copy-start | bytes 24580
  351.8 113.2 %reduce-scatter.11.cloned.1.call-start = ((), (), s32[]{:S(2)}) async-start(), calls=%async_computation.8 | async-start | bytes 6488064 | tf_op jit(solution)/shard_map/reduce_scatter | solution.py:53
  392.8 0.7 copy-start.16
  392.9 87.3 %reduce-scatter.13.cloned.1.call-start = ((), (), s32[]{:S(2)}) async-start(), calls=%async_computation.9 | async-start | bytes 6488064 | tf_op jit(solution)/shard_map/reduce_scatter | solution.py:53
  416.2 103.0 %reduce-scatter.7.cloned.1.call-start = ((), (), s32[]{:S(2)}) async-start(), calls=%async_computation.6 | async-start | bytes 6488064 | tf_op jit(solution)/shard_map/reduce_scatter | solution.py:53
  443.2 114.8 %reduce-scatter.9.cloned.1.call-start = ((), (), s32[]{:S(2)}) async-start(), calls=%async_computation.7 | async-start | bytes 6488064 | tf_op jit(solution)/shard_map/reduce_scatter | solution.py:53
  462.1 115.8 %copy-start.4 = (bf16[2,352,1024]{2,1,0:T(8,128)(2,1)S(1)}, bf16[2,352,1024]{2,1,0:T(8,128)(2,1)}, u32[]{:S(2)}) copy-start(bf16[2,352,1024]{2,1,0:T(8,128)(2,1)} %param.15) | copy-start | bytes 4325380
  557.9 26.7 %copy-start.13 = (bf16[128,2816]{1,0:T(8,128)(2,1)S(1)}, bf16[128,2816]{1,0:T(8,128)(2,1)}, u32[]{:S(2)}) copy-start(bf16[128,2816]{1,0:T(8,128)(2,1)} %reduce-scatter.7.cloned.1.call-done) | copy-start | bytes 2162692
  557.9 26.7 %copy-start.14 = (bf16[128,2816]{1,0:T(8,128)(2,1)S(1)}, bf16[128,2816]{1,0:T(8,128)(2,1)}, u32[]{:S(2)}) copy-start(bf16[128,2816]{1,0:T(8,128)(2,1)} %reduce-scatter.9.cloned.1.call-done) | copy-start | bytes 2162692
  577.9 6.8 %copy-start.1 = (bf16[2,128,2816]{2,1,0:T(8,128)(2,1)S(1)}, bf16[2,128,2816]{2,1,0:T(8,128)(2,1)}, u32[]{:S(2)}) copy-start(bf16[2,128,2816]{2,1,0:T(8,128)(2,1)} %param.13) | copy-start | bytes 4325380
  577.9 6.8 %copy-start.2 = (bf16[2,128,2816]{2,1,0:T(8,128)(2,1)S(1)}, bf16[2,128,2816]{2,1,0:T(8,128)(2,1)}, u32[]{:S(2)}) copy-start(bf16[2,128,2816]{2,1,0:T(8,128)(2,1)} %param.14) | copy-start | bytes 4325380
  577.9 6.7 %copy-start.7 = (f32[2,128,2816]{2,1,0:T(8,128)S(1)}, f32[2,128,2816]{2,1,0:T(8,128)}, u32[]{:S(2)}) copy-start(f32[2,128,2816]{2,1,0:T(8,128)} %param.19) | copy-start | bytes 8650756
  577.9 8.2 %copy-start.8 = (f32[2,128,2816]{2,1,0:T(8,128)S(1)}, f32[2,128,2816]{2,1,0:T(8,128)}, u32[]{:S(2)}) copy-start(f32[2,128,2816]{2,1,0:T(8,128)} %param.16) | copy-start | bytes 8650756
  577.9 9.0 %copy-start.9 = (f32[2,128,2816]{2,1,0:T(8,128)S(1)}, f32[2,128,2816]{2,1,0:T(8,128)}, u32[]{:S(2)}) copy-start(f32[2,128,2816]{2,1,0:T(8,128)} %param.20) | copy-start | bytes 8650756
  577.9 9.8 %copy-start.10 = (f32[2,128,2816]{2,1,0:T(8,128)S(1)}, f32[2,128,2816]{2,1,0:T(8,128)}, u32[]{:S(2)}) copy-start(f32[2,128,2816]{2,1,0:T(8,128)} %param.17) | copy-start | bytes 8650756
  577.9 9.9 %copy-start.11 = (bf16[128,2816]{1,0:T(8,128)(2,1)S(1)}, bf16[128,2816]{1,0:T(8,128)(2,1)}, u32[]{:S(2)}) copy-start(bf16[128,2816]{1,0:T(8,128)(2,1)} %reduce-scatter.11.cloned.1.call-done) | copy-start | bytes 2162692
  577.9 10.1 %copy-start.12 = (bf16[128,2816]{1,0:T(8,128)(2,1)S(1)}, bf16[128,2816]{1,0:T(8,128)(2,1)}, u32[]{:S(2)}) copy-start(bf16[128,2816]{1,0:T(8,128)(2,1)} %reduce-scatter.13.cloned.1.call-done) | copy-start | bytes 2162692
Sparse Core Ops, SparseCore 0:
  10.2 37.5 all-gather.12
  50.0 34.3 all-gather.14
  86.6 34.3 all-gather.16
  123.0 34.3 all-gather.20
  159.4 34.3 all-gather.22
  195.9 34.3 all-gather.18
  328.3 35.2 reduce-scatter.14
  365.9 36.5 reduce-scatter.16
  404.8 36.5 reduce-scatter.10
  443.6 36.5 reduce-scatter.12
  482.5 36.5 reduce-scatter.6
  521.3 36.5 reduce-scatter.8
where the time goes:
time: 613 us; the launch traced here: 602 us
  matrix products  331 us (54%)
  waiting for transfers between devices  185 us (30%)
  other arithmetic  28.3 us (5%)
  local copies, waits for them, and re-layouts  25.5 us (4%)
  between operations  17.6 us (3%)
  blocking collectives  14.5 us (2%)
    dot_general x5, matrix products, layer(): gate = jnp.dot(a, w['w_gate'], preferred_element_type=jnp.float32)  119 us
    dot_general x5, matrix products, layer(): up = jnp.dot(a, w['w_up'], preferred_element_type=jnp.float32)  115 us
    dot_general x5, matrix products, matmul(): jnp.dot(a, w, preferred_element_type=jnp.float32).astype(jnp.bfloat16)  97.1 us
    all_gather x6, waiting for transfers between devices, fetched(): lax.all_gather(w[number], 'dp', axis=0, tiled=True)  92.5 us
    reduce_scatter x6, waiting for transfers between devices, step(): lax.psum_scatter(by_w[name], 'dp', scatter_dimension=0, tiled=True)  90.3 us
    unnamed x44, local copies, waits for them, and re-layouts  19.1 us
    psum x1, blocking collectives, step(): squares = lax.psum(sum((jnp.sum(g * g) for g in gradients)), 'dp')  14.5 us
    convert_element_type x2, other arithmetic, adamw(): return ((w - 0.02 * step).astype(jnp.bfloat16), m, v)  13.4 us
  transfers between devices with their start and end apart: 12, of which 9 were waited for; matrix products, arithmetic and copies ran while one was open for 44% of the time, Pallas kernels for 0%

commit v1 on v0

v1 whole, which is shorter than its diff:
```python
import functools

import jax
import jax.numpy as jnp
from jax import lax
from jax.experimental import pallas as pl
from jax.experimental.pallas import tpu as pltpu
from jax.sharding import PartitionSpec as P

MESH = pl.DeviceIdType.MESH
F32, BF16 = jnp.float32, jnp.bfloat16
ROWS = 32
BLOCK = 512
OWN, DEEP = 4, 3


def dot(a, b):
    return lax.dot_general(a, b, (((1,), (0,)), ((), ())), preferred_element_type=F32)


def dot_t(a, b):
    return lax.dot_general(a, b, (((1,), (1,)), ((), ())), preferred_element_type=F32)


def kernel(
    n, count,
    x, dy, wg, wu, wd,
    gath, act_st, sgu_st, a0t_st, gg, gu, gd, fac,
    va, vat, vc, vct, acc, act, sgu, dgu, wgu_b, wd_b,
    own, term, pair, part, fin, halves, wholes, squares, norms,
    in_sem, own_send, own_local, full_recv, half_recv, part_recv, fwd_send, load_sem, stash_sem, saved_sem,
    pair_send, pair_recv, b_send, b_recv, c_send, c_recv, norm_send, norm_recv,
    pair_free, b_free, c_free,
):
    me = lax.axis_index("dp")
    chips = n // 2
    c, at = lax.rem(me, 2), lax.div(me, 2)
    over = lax.rem(at + 2, chips)
    right_chip, left_chip = lax.rem(at + 1, chips), lax.rem(at + chips - 1, chips)
    partner = at * 2 + 1 - c
    right, left, far = right_chip * 2 + c, left_chip * 2 + c, over * 2 + c
    tokens, d = va.shape
    wide = wgu_b.shape[3] // 2
    slots = wd.shape[1] // ROWS
    layers = wd.shape[0]
    chunks = layers * slots
    blocks = tokens // BLOCK
    high = own.shape[1]
    mid = high // 2
    tall = wg.shape[1]

    def remote(src, dst, send, recv, to):
        return pltpu.make_async_remote_copy(
            src_ref=src, dst_ref=dst, send_sem=send, recv_sem=recv, device_id={"dp": to}, device_id_type=MESH
        )

    def prepare(k):
        b, layer, s = lax.rem(k, OWN), lax.div(k, slots), lax.rem(k, slots)
        lanes = lax.broadcasted_iota(jnp.int32, (tall, 128), 1) // ROWS
        for w, base in ((wg, 0), (wu, wide)):
            for group in range(n // 4):
                total = None
                for place in range(4):
                    unit = slots * (4 * group + place) + s
                    piece = w[layer, :, pl.ds(pl.multiple_of(lax.div(unit, 4) * 128, 128), 128)].astype(F32)
                    piece = pltpu.roll(piece, lax.rem(place + 4 - lax.rem(unit, 4), 4) * ROWS, 1)
                    total = piece if total is None else jnp.where(lanes == place, piece, total)
                own[b, 0:tall, base + 128 * group : base + 128 * (group + 1)] = total.astype(BF16)
        rows = wd[layer, pl.ds(pl.multiple_of(s * ROWS, ROWS), ROWS), :]
        own[b, tall : tall + ROWS, :] = rows[:, : 2 * wide]
        own[b, tall + ROWS : high, :] = rows[:, 2 * wide :]

    def own_copies(k):
        b = lax.rem(k, OWN)
        return [
            remote(own.at[b], gath.at[k, me], own_send.at[b, 0], full_recv.at[b, 0], right),
            remote(own.at[b], gath.at[k, me], own_send.at[b, 1], full_recv.at[b, 1], left),
            remote(own.at[b], gath.at[k, me], own_send.at[b, 2], part_recv.at[b, 0], partner),
        ]

    def own_here(k):
        b = lax.rem(k, OWN)
        return pltpu.make_async_copy(own.at[b], gath.at[k, me], own_local.at[b])

    def e1(k):
        for copy in own_copies(k):
            copy.start()
        own_here(k).start()

        @pl.when(k + 1 < chunks)
        def _():
            @pl.when(k + 1 >= OWN)
            def _():
                for copy in own_copies(k + 1 - OWN):
                    copy.wait_send()

            prepare(k + 1)

    def arrived(region, recv):
        remote(region, region, fwd_send.at[0, 0], recv, me).wait_recv()

    def forwards(k):
        b = lax.rem(k, OWN)
        return [
            remote(gath.at[k, left, 0:mid], gath.at[k, left, 0:mid], fwd_send.at[b, 0], half_recv.at[b, 0], right),
            remote(gath.at[k, right, mid:high], gath.at[k, right, mid:high], fwd_send.at[b, 1], half_recv.at[b, 1], left),
            remote(gath.at[k, left], gath.at[k, left], fwd_send.at[b, 2], part_recv.at[b, 1], partner),
            remote(gath.at[k, right], gath.at[k, right], fwd_send.at[b, 3], part_recv.at[b, 2], partner),
        ]

    def last_forward(k):
        b = lax.rem(k, OWN)
        return remote(gath.at[k, far], gath.at[k, far], fwd_send.at[b, 4], part_recv.at[b, 3], partner)

    def e2(k):
        b = lax.rem(k, OWN)

        @pl.when(k >= OWN)
        def _():
            for copy in forwards(k - OWN):
                copy.wait_send()

        arrived(gath.at[k, left], full_recv.at[b, 0])
        arrived(gath.at[k, right], full_recv.at[b, 1])
        for copy in forwards(k):
            copy.start()

    def e3(k):
        b = lax.rem(k, OWN)

        @pl.when(k >= OWN)
        def _():
            last_forward(k - OWN).wait_send()

        arrived(gath.at[k, far, 0:mid], half_recv.at[b, 0])
        arrived(gath.at[k, far, mid:high], half_recv.at[b, 1])
        last_forward(k).start()

    def down_loads(k, b):
        return [
            pltpu.make_async_copy(gath.at[k, :, tall : tall + ROWS], wd_b.at[b, :, :, 0 : 2 * wide], load_sem.at[b, 0]),
            pltpu.make_async_copy(gath.at[k, :, tall + ROWS : high], wd_b.at[b, :, :, 2 * wide : 4 * wide], load_sem.at[b, 1]),
        ]

    def loads(k):
        b = lax.rem(k, 2)
        return [pltpu.make_async_copy(gath.at[k, :, 0:tall], wgu_b.at[b], load_sem.at[b, 2])] + down_loads(k, b)

    def e4(k):
        b = lax.rem(k, OWN)
        other = 1 - 2 * c
        own_here(k).wait()
        for i, j in enumerate((me, left, right, far)):
            arrived(gath.at[k, j + other], part_recv.at[b, i])
        for copy in loads(k):
            copy.start()

    def pair_copy(r):
        b = lax.rem(r, 2)
        return remote(term.at[b, 1 - c], pair.at[b], pair_send.at[b], pair_recv.at[b], partner)

    def b_copies(r):
        b = lax.rem(r, DEEP)
        return [
            remote(part.at[b, 1, 0:mid], halves.at[b, 0], b_send.at[b, 0], b_recv.at[b, 0], right),
            remote(part.at[b, 1, mid:high], halves.at[b, 1], b_send.at[b, 1], b_recv.at[b, 1], left),
        ]

    def c_copies(r):
        b = lax.rem(r, DEEP)
        return [
            remote(part.at[b, 0], wholes.at[b, 0], c_send.at[b, 0], c_recv.at[b, 0], right),
            remote(part.at[b, 2], wholes.at[b, 1], c_send.at[b, 1], c_recv.at[b, 1], left),
        ]

    def free(sem, to):
        pl.semaphore_signal(sem, inc=1, device_id={"dp": to}, device_id_type=MESH)

    STRIP = 48

    def f1(r):
        @pl.when(r >= 2)
        def _():
            pl.semaphore_wait(pair_free, 1)

        pair_copy(r).start()

    def f2(r):
        b, p = lax.rem(r, DEEP), lax.rem(r, 2)

        @pl.when(r >= DEEP)
        def _():
            for copy in b_copies(r - DEEP) + c_copies(r - DEEP):
                copy.wait_send()
            pl.semaphore_wait(b_free.at[0], 1)
            pl.semaphore_wait(b_free.at[1], 1)

        pair_copy(r).wait_recv()
        for away, chip in ((2, over), (1, right_chip), (3, left_chip), (0, at)):
            for row in range(0, high, STRIP):
                total = term[p, c, chip, row : row + STRIP, :].astype(F32) + pair[p, chip, row : row + STRIP, :].astype(F32)
                if away:
                    part[b, away - 1, row : row + STRIP, :] = total.astype(BF16)
                else:
                    fin[b, row : row + STRIP, :] = total
        for copy in b_copies(r):
            copy.start()
        pair_copy(r).wait_send()

        @pl.when(r + 2 < chunks)
        def _():
            free(pair_free, partner)

    def f3(r):
        b = lax.rem(r, DEEP)

        @pl.when(r >= DEEP)
        def _():
            pl.semaphore_wait(c_free.at[0], 1)
            pl.semaphore_wait(c_free.at[1], 1)

        for i in range(2):
            b_copies(r)[i].wait_recv()
            start = mid * i
            for row in range(0, mid, STRIP):
                total = part[b, 2 * i, start + row : start + row + STRIP, :].astype(F32) + halves[b, i, row : row + STRIP, :].astype(F32)
                part[b, 2 * i, start + row : start + row + STRIP, :] = total.astype(BF16)

        @pl.when(r + DEEP < chunks)
        def _():
            free(b_free.at[0], left)
            free(b_free.at[1], right)

        for copy in c_copies(r):
            copy.start()

    def f4(r):
        b = lax.rem(r, DEEP)
        layer, s = 1 - lax.div(r, slots), lax.rem(r, slots)
        for copy in c_copies(r):
            copy.wait_recv()
        lanes = lax.broadcasted_iota(jnp.int32, (tall, 128), 1) // ROWS
        out = squares[...]
        for half, grad in ((0, gg), (1, gu)):
            for group in range(n // 4):
                cols = slice(half * wide + 128 * group, half * wide + 128 * (group + 1))
                total = fin[b, 0:tall, cols] + wholes[b, 0, 0:tall, cols].astype(F32) + wholes[b, 1, 0:tall, cols].astype(F32)
                total = total.astype(BF16).astype(F32)
                out = out + jnp.sum((total * total).reshape(tall // 8, 8, 128), axis=0)
                for place in range(4):
                    unit = slots * (4 * group + place) + s
                    where = pl.ds(pl.multiple_of(lax.div(unit, 4) * 128, 128), 128)
                    moved = pltpu.roll(total, lax.rem(lax.rem(unit, 4) + 4 - place, 4) * ROWS, 1)
                    grad[layer, :, where] = jnp.where(lanes == lax.rem(unit, 4), moved, grad[layer, :, where].astype(F32)).astype(BF16)
        for half in range(2):
            rows = slice(tall + ROWS * half, tall + ROWS * (half + 1))
            total = fin[b, rows, :] + wholes[b, 0, rows, :].astype(F32) + wholes[b, 1, rows, :].astype(F32)
            total = total.astype(BF16).astype(F32)
            gd[layer, pl.ds(pl.multiple_of(s * ROWS, ROWS), ROWS), 2 * wide * half : 2 * wide * (half + 1)] = total.astype(BF16)
            for lane in range(0, 2 * wide, 128):
                one = total[:, lane : lane + 128]
                out = out + jnp.sum((one * one).reshape(ROWS // 8, 8, 128), axis=0)
        squares[...] = out

        @pl.when(r + DEEP < chunks)
        def _():
            free(c_free.at[0], left)
            free(c_free.at[1], right)

    def turn(block, dst, start, size):
        for q in range(0, d, 256):
            dst[q : q + 256, pl.ds(start, size)] = block[:, q : q + 256].T.astype(BF16)

    def gates(rows, b):
        both = dot(va[rows, :], wgu_b[b].reshape(d, 2 * wide))
        g, u = both[:, :wide], both[:, wide:]
        sig = jax.nn.sigmoid(g)
        silu = g * sig
        return silu, u * (sig + silu * (1.0 - sig)), (silu * u).astype(BF16)

    def gradients(r, a):
        p = lax.rem(r, 2)
        for m in range(2):
            g = dot(vat[512 * m : 512 * (m + 1), :], dgu[...]).astype(BF16)
            for i in range(512 // tall):
                j = m * (512 // tall) + i
                term[p, j % 2, j // 2, 0:tall, :] = g[tall * i : tall * (i + 1), :]
        hidden = act[a]
        for m in range(4):
            g = dot(vct[256 * m : 256 * (m + 1), :], hidden).T.astype(BF16)
            low = tall + ROWS * (m // 2)
            for j in range(n):
                term[p, j % 2, j // 2, low : low + ROWS, 256 * (m % 2) : 256 * (m % 2 + 1)] = g[ROWS * j : ROWS * (j + 1), :]

    def stashes(t, b):
        return [
            pltpu.make_async_copy(act.at[b], act_st.at[t], stash_sem.at[b, 0]),
            pltpu.make_async_copy(sgu.at[b], sgu_st.at[t], stash_sem.at[b, 1]),
        ]

    def saved(s):
        b = lax.rem(s, 2)
        return down_loads(s, b) + [
            pltpu.make_async_copy(act_st.at[s], act.at[b], saved_sem.at[b, 0]),
            pltpu.make_async_copy(sgu_st.at[s], sgu.at[b], saved_sem.at[b, 1]),
        ]

    x_in = pltpu.make_async_copy(x, va, in_sem.at[0])
    dy_in = pltpu.make_async_copy(dy, vc, in_sem.at[1])
    x_in.start()
    dy_in.start()
    barrier = pltpu.get_barrier_semaphore()
    for i in range(1, n):
        pl.semaphore_signal(barrier, inc=1, device_id={"dp": lax.rem(me + i, n)}, device_id_type=MESH)
    prepare(0)
    pl.semaphore_wait(barrier, n - 1)
    e1(0)
    e1(1)
    x_in.wait()

    def first(i, _):
        start = pl.multiple_of(i * 256, 256)
        rows = pl.ds(start, 256)
        h = va[rows, :].astype(F32)
        a = (h * lax.rsqrt(jnp.mean(h * h, -1, keepdims=True) + 1e-6)).astype(BF16)
        va[rows, :] = a
        turn(a.astype(F32), vat, start, 256)
        acc[rows, :] = jnp.zeros((256, d), F32)
        return 0

    lax.fori_loop(0, tokens // 256, first, 0)
    a0t_out = pltpu.make_async_copy(vat, a0t_st, in_sem.at[2])
    a0t_out.start()
    e2(0)
    e1(2)
    dy_in.wait()

    def second(i, _):
        start = pl.multiple_of(i * 256, 256)
        turn(vc[pl.ds(start, 256), :].astype(F32), vct, start, 256)
        return 0

    lax.fori_loop(0, tokens // 256, second, 0)
    e3(0)
    e2(1)
    e4(0)
    gg[...] = jnp.zeros_like(gg)
    gu[...] = jnp.zeros_like(gu)
    squares[...] = jnp.zeros_like(squares)

    def forward(t, _):
        e1(t + 3)
        e3(t + 1)
        for copy in loads(t):
            copy.wait()
        b = lax.rem(t, 2)

        @pl.when(t >= 2)
        def _():
            for copy in stashes(t - 2, b):
                copy.wait()

        def work(i, _):
            rows = pl.ds(pl.multiple_of(i * BLOCK, BLOCK), BLOCK)
            silu, slope, hidden = gates(rows, b)
            act[b, rows, :] = hidden
            sgu[b, rows, 0:wide] = slope
            sgu[b, rows, wide:] = silu
            acc[rows, :] += dot(hidden, wd_b[b].reshape(n * ROWS, d))
            return 0

        lax.fori_loop(0, blocks // 2, work, 0)
        e2(t + 2)
        e4(t + 1)
        lax.fori_loop(blocks // 2, blocks, work, 0)
        for copy in stashes(t, b):
            copy.start()
        return 0

    lax.fori_loop(0, slots, forward, 0)
    x_in.start()
    a0t_out.wait()
    for t in (slots - 2, slots - 1):
        for copy in stashes(t, t % 2):
            copy.wait()
    x_in.wait()

    def between(i, _):
        start = pl.multiple_of(i * 256, 256)
        rows = pl.ds(start, 256)
        h = (va[rows, :].astype(F32) + acc[rows, :].astype(BF16).astype(F32)).astype(BF16).astype(F32)
        sgu[0, rows, :] = h[:, : 2 * wide]
        sgu[1, rows, :] = h[:, 2 * wide :]
        a = (h * lax.rsqrt(jnp.mean(h * h, -1, keepdims=True) + 1e-6)).astype(BF16)
        va[rows, :] = a
        turn(a.astype(F32), vat, start, 256)
        acc[rows, :] = jnp.zeros((256, d), F32)
        return 0

    lax.fori_loop(0, tokens // 256, between, 0)

    def both_ways(t, _):
        r = t - slots

        @pl.when(t + 3 < chunks)
        def _():
            e1(t + 3)

        @pl.when(t + 1 < chunks)
        def _():
            e3(t + 1)

        for copy in loads(t):
            copy.wait()
        b = lax.rem(t, 2)

        def work(i, _):
            rows = pl.ds(pl.multiple_of(i * BLOCK, BLOCK), BLOCK)
            silu, slope, hidden = gates(rows, b)
            by = dot_t(vc[rows, :], wd_b[b].reshape(n * ROWS, d)).astype(BF16).astype(F32)
            act[0, rows, :] = hidden
            dg, du = (by * slope).astype(BF16), (by * silu).astype(BF16)
            dgu[rows, 0:wide] = dg
            dgu[rows, wide:] = du
            acc[rows, :] += dot_t(jnp.concatenate([dg, du], axis=1), wgu_b[b].reshape(d, 2 * wide))
            return 0

        lax.fori_loop(0, blocks, work, 0)

        @pl.when(r >= 1)
        def _():
            f2(r - 1)

        @pl.when(r >= 2)
        def _():
            f3(r - 2)

        @pl.when(t + 2 < chunks)
        def _():
            e2(t + 2)

        @pl.when(t + 1 < chunks)
        def _():
            e4(t + 1)

        @pl.when(r >= 3)
        def _():
            f4(r - 3)

        gradients(r, 0)
        f1(r)
        return 0

    lax.fori_loop(slots, chunks, both_ways, 0)
    a0t_in = pltpu.make_async_copy(a0t_st, vat, in_sem.at[2])
    a0t_in.start()

    def back(i, _):
        start = pl.multiple_of(i * 256, 256)
        rows = pl.ds(start, 256)
        h = jnp.concatenate([sgu[0, rows, :], sgu[1, rows, :]], axis=1)
        da = acc[rows, :].astype(BF16).astype(F32)
        scale = lax.rsqrt(jnp.mean(h * h, -1, keepdims=True) + 1e-6)
        along = jnp.mean(da * h, -1, keepdims=True)
        by_h = (da * scale - h * (scale * scale * scale * along)).astype(BF16).astype(F32)
        by_h = (vc[rows, :].astype(F32) + by_h).astype(BF16)
        vc[rows, :] = by_h
        turn(by_h.astype(F32), vct, start, 256)
        return 0

    lax.fori_loop(0, tokens // 256, back, 0)
    for copy in saved(0):
        copy.start()
    a0t_in.wait()

    def backward(t, _):
        r, s = t - slots, t - chunks
        b = lax.rem(s, 2)
        for copy in saved(s):
            copy.wait()

        @pl.when(s + 1 < slots)
        def _():
            for copy in saved(s + 1):
                copy.start()

        def work(i, _):
            rows = pl.ds(pl.multiple_of(i * BLOCK, BLOCK), BLOCK)
            by = dot_t(vc[rows, :], wd_b[b].reshape(n * ROWS, d)).astype(BF16).astype(F32)
            dgu[rows, 0:wide] = (by * sgu[b, rows, 0:wide]).astype(BF16)
            dgu[rows, wide:] = (by * sgu[b, rows, wide:]).astype(BF16)
            return 0

        lax.fori_loop(0, blocks, work, 0)
        f2(r - 1)
        f3(r - 2)
        f4(r - 3)
        gradients(r, b)
        f1(r)
        return 0

    lax.fori_loop(chunks, chunks + slots, backward, 0)

    f2(chunks - 1)
    f3(chunks - 2)
    f4(chunks - 3)
    f3(chunks - 1)
    f4(chunks - 2)
    f4(chunks - 1)
    for k in range(chunks - OWN, chunks):
        for copy in own_copies(k) + forwards(k) + [last_forward(k)]:
            copy.wait_send()
    for r in range(chunks - DEEP, chunks):
        for copy in b_copies(r) + c_copies(r):
            copy.wait_send()

    norms[me] = squares[...]
    sends = [
        remote(squares, norms.at[me], norm_send.at[i], norm_recv.at[i], lax.rem(me + i + 1, n)) for i in range(n - 1)
    ]
    for copy in sends:
        copy.start()
    for i in range(n - 1):
        source = lax.rem(me + n - i - 1, n)
        remote(norms.at[source], norms.at[source], norm_send.at[i], norm_recv.at[i], me).wait_recv()
    for copy in sends:
        copy.wait_send()
    total = jnp.sum(norms[...])
    fac[...] = jnp.minimum(1.0, 0.5 * lax.rsqrt(jnp.full(fac.shape, total / count, F32) + 1e-30))


def gradients_of(n, x, dy, wg, wu, wd):
    layers, tall, ff = wg.shape
    down, d = wd.shape[1:]
    tokens = x.shape[0]
    slots, wide = down // ROWS, n * ROWS
    chunks, high = layers * slots, tall + 2 * ROWS
    chips = n // 2
    assert layers == 2 and chips == 4 and d == 4 * wide and tokens % BLOCK == 0 and down % ROWS == 0
    hbm, vmem = pl.BlockSpec(memory_space=pl.ANY), pl.BlockSpec(memory_space=pltpu.VMEM)
    dma, plain = pltpu.SemaphoreType.DMA, pltpu.SemaphoreType.REGULAR
    out = pl.pallas_call(
        functools.partial(kernel, n, float(n * (wg.size + wu.size + wd.size))),
        out_shape=(
            jax.ShapeDtypeStruct((chunks, n, high, 2 * wide), BF16),
            jax.ShapeDtypeStruct((slots, tokens, wide), BF16),
            jax.ShapeDtypeStruct((slots, tokens, 2 * wide), F32),
            jax.ShapeDtypeStruct((d, tokens), BF16),
            jax.ShapeDtypeStruct(wg.shape, BF16),
            jax.ShapeDtypeStruct(wu.shape, BF16),
            jax.ShapeDtypeStruct(wd.shape, BF16),
            jax.ShapeDtypeStruct((8, 128), F32),
        ),
        in_specs=[hbm, hbm, vmem, vmem, vmem],
        out_specs=(hbm, hbm, hbm, hbm, vmem, vmem, vmem, vmem),
        scratch_shapes=[
            pltpu.VMEM((tokens, d), BF16),
            pltpu.VMEM((d, tokens), BF16),
            pltpu.VMEM((tokens, d), BF16),
            pltpu.VMEM((d, tokens), BF16),
            pltpu.VMEM((tokens, d), F32),
            pltpu.VMEM((2, tokens, wide), BF16),
            pltpu.VMEM((2, tokens, 2 * wide), F32),
            pltpu.VMEM((tokens, 2 * wide), BF16),
            pltpu.VMEM((2, n, tall, 2 * wide), BF16),
            pltpu.VMEM((2, n, ROWS, d), BF16),
            pltpu.VMEM((OWN, high, 2 * wide), BF16),
            pltpu.VMEM((2, 2, chips, high, 2 * wide), BF16),
            pltpu.VMEM((2, chips, high, 2 * wide), BF16),
            pltpu.VMEM((DEEP, 3, high, 2 * wide), BF16),
            pltpu.VMEM((DEEP, high, 2 * wide), F32),
            pltpu.VMEM((DEEP, 2, high // 2, 2 * wide), BF16),
            pltpu.VMEM((DEEP, 2, high, 2 * wide), BF16),
            pltpu.VMEM((8, 128), F32),
            pltpu.VMEM((n, 8, 128), F32),
            dma((3,)),
            dma((OWN, 3)),
            dma((OWN,)),
            dma((OWN, 2)),
            dma((OWN, 2)),
            dma((OWN, 4)),
            dma((OWN, 5)),
            dma((2, 3)),
            dma((2, 2)),
            dma((2, 2)),
            dma((2,)),
            dma((2,)),
            dma((DEEP, 2)),
            dma((DEEP, 2)),
            dma((DEEP, 2)),
            dma((DEEP, 2)),
            dma((n - 1,)),
            dma((n - 1,)),
            plain,
            plain((2,)),
            plain((2,)),
        ],
        compiler_params=pltpu.CompilerParams(collective_id=0, has_side_effects=True, vmem_limit_bytes=67043328),
        cost_estimate=pl.CostEstimate(
            flops=30 * tokens * d * ff, bytes_accessed=200_000_000, transcendentals=2 * layers * tokens * ff
        ),
    )(x, dy, wg, wu, wd)
    return out[4:7], out[7][0, 0]


def adamw(w, m, v, g):
    m = 0.9 * m + 0.1 * g
    v = 0.95 * v + 0.05 * g * g
    step = m * lax.rsqrt(v + 1e-8) + 0.1 * w
    return (w - 0.02 * step).astype(BF16), m, v


def solution(mesh):
    n = mesh.shape["dp"]

    def step(x, dy, *arrays):
        weights, m, v = (arrays[i : i + 3] for i in (0, 3, 6))
        gradients, factor = gradients_of(n, x[0], dy[0], *weights)
        new = [
            adamw(w.astype(F32), m, v, g.astype(F32) * factor) for w, m, v, g in zip(weights, m, v, gradients, strict=True)
        ]
        return tuple(one[which] for which in range(3) for one in new)

    states, cut = P(("rep", "dp"), None, None), P(None, "dp", None)
    return jax.shard_map(
        step,
        mesh=mesh,
        in_specs=(states, states) + (cut,) * 9,
        out_specs=(P("rep", "dp", None),) * 9,
        check_vma=False,
    )
```

time: 613 us -> 407 us (0.66); the launches traced: 602 us -> 407 us
  Pallas kernels: 0 us -> 387 us
  matrix products: 331 us -> 0 us
  waiting for transfers between devices: 185 us -> 0 us
  local copies, waits for them, and re-layouts: 25.5 us -> 2.65 us
  between operations: 17.6 us -> 0.7 us
  blocking collectives: 14.5 us -> 0 us
  other arithmetic: 28.3 us -> 16.8 us
    pallas_call x0 -> x1, Pallas kernels: none -> 387 us  [gradients_of(): pl.pallas_call(functools.partial(kernel, n, float(n * (wg.size + wu.size...]
    dot_general x15 -> x0, matrix products: 331 us -> none  [the longest x5 119 us: layer(): gate = jnp.dot(a, w['w_gate'], preferred_element_type=jnp.float32)]
    all_gather x6 -> x0, waiting for transfers between devices: 92.5 us -> none  [fetched(): lax.all_gather(w[number], 'dp', axis=0, tiled=True)]
    reduce_scatter x6 -> x0, waiting for transfers between devices: 90.3 us -> none  [step(): lax.psum_scatter(by_w[name], 'dp', scatter_dimension=0, tiled=True)]
    unnamed x44 -> x14, local copies, waits for them, and re-layouts: 19.1 us -> 1.41 us
    psum x1 -> x0, blocking collectives: 14.5 us -> none  [step(): squares = lax.psum(sum((jnp.sum(g * g) for g in gradients)), 'dp')]
    reduce_sum x4 -> x0, other arithmetic: 11.3 us -> none  [the longest x3 8.22 us: step(): squares = lax.psum(sum((jnp.sum(g * g) for g in gradients)), 'dp')]
  transfers between devices with their start and end apart: 12 -> 0, of which waited for: 9 -> 0; matrix products, arithmetic and copies ran while one was open for 44% -> 0% of each run, Pallas kernels for 0% -> 0%
where the time goes in v1:
time: 407 us
  Pallas kernels  387 us (95%)
  other arithmetic  16.8 us (4%)
    pallas_call x1, Pallas kernels, gradients_of(): pl.pallas_call(functools.partial(kernel, n, float(n * (wg.size + wu.size...  387 us
    convert_element_type x2, other arithmetic, adamw(): return ((w - 0.02 * step).astype(BF16), m, v)  16.8 us

profile of v1, /device:TPU:113, one launch (start us, length us, event | category | flops | bytes accessed | tf_op | source)
XLA Modules:
  0.0 407.2 jit_solution(6747276997012918875)
XLA Ops:
  0.6 387.1 %shard_map.178 = (bf16[22,8,192,512]{3,2,1,0:T(8,128)(2,1)}, bf16[11,2048,256]{2,1,0:T(8,128)(2,1)}, f32[11,2048,512]{2,1,0:T(8,128)}, bf16[1024,2048]{1,0:T(8,1...) custom-call(bf16[2048,1024]{1,0:T(8,128)(2,1)} %bitcast.3, ...), custom_call_target="tpu_custom_call" | custom-call | flops 177167400960 | bytes 200000000 | tf_op jit(solution)/shard_map/pallas_call | solution.py:542
  387.7 1.2 slice.3
  388.9 0.0 copy-start
  388.9 0.0 copy-start.1
  389.0 0.0 copy-start.2
  389.0 0.0 copy-start.3
  389.0 0.0 copy-start.4
  389.0 0.0 copy-start.5
  389.0 0.0 copy-start.6
  389.0 9.2 %fusion.8 = (bf16[2,352,1024]{2,1,0:T(8,128)(2,1)}, f32[2,352,1024]{2,1,0:T(8,128)}, f32[2,352,1024]{2,1,0:T(8,128)}) fusion(bf16[2,352,1024]{2,1,0:T(8,128)(2,1)} %wd.1, f32[]{:T(128)} %bitcast.2, bf16[2,352,1024]{2,1,0:T(8,128)(2,1)} %get-tuple-element.16, f32[2,352,1024]{2,1,0:T(8,128)} %param.21, f32[2,352,1024]{2,1,0:T(8,128)} %param.18), kind=kLoop, calls=%fused_computation.17 | loop fusion | flops 12255232 | bytes 15859716 | tf_op jit(solution)/shard_map/convert_element_type | solution.py:610
  398.2 0.0 copy-done
  398.2 0.0 copy-done.1
  398.2 0.0 copy-done.2
  398.2 0.0 copy-done.3
  398.2 0.0 copy-done.4
  398.2 1.0 copy-done.5
  399.2 0.4 copy-done.6
  399.6 7.6 %fusion.2 = (bf16[2,128,2816]{2,1,0:T(8,128)(2,1)}, f32[2,128,2816]{2,1,0:T(8,128)}, f32[2,128,2816]{2,1,0:T(8,128)}, bf16[2,128,2816]{2,1,0:T(8,128)(2,1)}, f32...) fusion(bf16[2,128,2816]{2,1,0:T(8,128)(2,1)S(1)} %copy-done.4, f32[]{:T(128)} %bitcast.2, ...), kind=kLoop, calls=%fused_computation.11 | loop fusion | flops 24510464 | bytes 31719428 | tf_op jit(solution)/shard_map/convert_element_type | solution.py:610
Async XLA Ops:
  388.9 9.2 %copy-start = (f32[2,128,2816]{2,1,0:T(8,128)S(1)}, f32[2,128,2816]{2,1,0:T(8,128)}, u32[]{:S(2)}) copy-start(f32[2,128,2816]{2,1,0:T(8,128)} %param.19) | copy-start | bytes 8650756
  388.9 9.2 %copy-start.1 = (f32[2,128,2816]{2,1,0:T(8,128)S(1)}, f32[2,128,2816]{2,1,0:T(8,128)}, u32[]{:S(2)}) copy-start(f32[2,128,2816]{2,1,0:T(8,128)} %param.16) | copy-start | bytes 8650756
  389.0 9.2 %copy-start.2 = (f32[2,128,2816]{2,1,0:T(8,128)S(1)}, f32[2,128,2816]{2,1,0:T(8,128)}, u32[]{:S(2)}) copy-start(f32[2,128,2816]{2,1,0:T(8,128)} %param.20) | copy-start | bytes 8650756
  389.0 9.2 %copy-start.3 = (f32[2,128,2816]{2,1,0:T(8,128)S(1)}, f32[2,128,2816]{2,1,0:T(8,128)}, u32[]{:S(2)}) copy-start(f32[2,128,2816]{2,1,0:T(8,128)} %param.17) | copy-start | bytes 8650756
  389.0 9.2 %copy-start.4 = (bf16[2,128,2816]{2,1,0:T(8,128)(2,1)S(1)}, bf16[2,128,2816]{2,1,0:T(8,128)(2,1)}, u32[]{:S(2)}) copy-start(bf16[2,128,2816]{2,1,0:T(8,128)(2,1)} %wg.1) | copy-start | bytes 4325380
  389.0 10.2 %copy-start.5 = (bf16[2,128,2816]{2,1,0:T(8,128)(2,1)S(1)}, bf16[2,128,2816]{2,1,0:T(8,128)(2,1)}, u32[]{:S(2)}) copy-start(bf16[2,128,2816]{2,1,0:T(8,128)(2,1)} %wu.1) | copy-start | bytes 4325380
  389.0 10.6 %copy-start.6 = (bf16[2,128,2816]{2,1,0:T(8,128)(2,1)S(1)}, bf16[2,128,2816]{2,1,0:T(8,128)(2,1)}, u32[]{:S(2)}) copy-start(bf16[2,128,2816]{2,1,0:T(8,128)(2,1)} %get-tuple-element.13) | copy-start | bytes 4325380

commit v2 on v1

--- a/solution.py
+++ b/solution.py
@@ -11,7 +11,7 @@
 F32, BF16 = jnp.float32, jnp.bfloat16
 ROWS = 32
 BLOCK = 512
-OWN, DEEP = 4, 3
+OWN, DEEP = 6, 3
 
 
 def dot(a, b):
@@ -343,14 +343,16 @@
     lax.fori_loop(0, tokens // 256, second, 0)
     e3(0)
     e2(1)
+    e1(3)
     e4(0)
     gg[...] = jnp.zeros_like(gg)
     gu[...] = jnp.zeros_like(gu)
     squares[...] = jnp.zeros_like(squares)
 
     def forward(t, _):
-        e1(t + 3)
+        e2(t + 2)
         e3(t + 1)
+        e1(t + 4)
         for copy in loads(t):
             copy.wait()
         b = lax.rem(t, 2)
@@ -370,7 +372,6 @@
             return 0
 
         lax.fori_loop(0, blocks // 2, work, 0)
-        e2(t + 2)
         e4(t + 1)
         lax.fori_loop(blocks // 2, blocks, work, 0)
         for copy in stashes(t, b):
@@ -402,13 +403,17 @@
     def both_ways(t, _):
         r = t - slots
 
-        @pl.when(t + 3 < chunks)
-        def _():
-            e1(t + 3)
+        @pl.when(t + 2 < chunks)
+        def _():
+            e2(t + 2)
 
         @pl.when(t + 1 < chunks)
         def _():
             e3(t + 1)
+
+        @pl.when(t + 4 < chunks)
+        def _():
+            e1(t + 4)
 
         for copy in loads(t):
             copy.wait()
@@ -427,6 +432,14 @@
 
         lax.fori_loop(0, blocks, work, 0)
 
+        @pl.when(t + 1 < chunks)
+        def _():
+            e4(t + 1)
+
+        @pl.when(r >= 4)
+        def _():
+            f4(r - 4)
+
         @pl.when(r >= 1)
         def _():
             f2(r - 1)
@@ -434,18 +447,6 @@
         @pl.when(r >= 2)
         def _():
             f3(r - 2)
-
-        @pl.when(t + 2 < chunks)
-        def _():
-            e2(t + 2)
-
-        @pl.when(t + 1 < chunks)
-        def _():
-            e4(t + 1)
-
-        @pl.when(r >= 3)
-        def _():
-            f4(r - 3)
 
         gradients(r, 0)
         f1(r)
@@ -454,6 +455,8 @@
     lax.fori_loop(slots, chunks, both_ways, 0)
     a0t_in = pltpu.make_async_copy(a0t_st, vat, in_sem.at[2])
     a0t_in.start()
+    for copy in saved(0)[:3]:
+        copy.start()
 
     def back(i, _):
         start = pl.multiple_of(i * 256, 256)
@@ -469,8 +472,7 @@
         return 0
 
     lax.fori_loop(0, tokens // 256, back, 0)
-    for copy in saved(0):
-        copy.start()
+    saved(0)[3].start()
     a0t_in.wait()
 
     def backward(t, _):
@@ -492,15 +494,16 @@
             return 0
 
         lax.fori_loop(0, blocks, work, 0)
+        f4(r - 4)
         f2(r - 1)
         f3(r - 2)
-        f4(r - 3)
         gradients(r, b)
         f1(r)
         return 0
 
     lax.fori_loop(chunks, chunks + slots, backward, 0)
 
+    f4(chunks - 4)
     f2(chunks - 1)
     f3(chunks - 2)
     f4(chunks - 3)

time: 407 us -> 362 us (0.89)
  Pallas kernels: 387 us -> 342 us
    pallas_call x1, Pallas kernels: 387 us -> 342 us  [gradients_of(): pl.pallas_call(functools.partial(kernel, n, float(n * (wg.size + wu.size...]
where the time goes in v2:
time: 362 us
  Pallas kernels  342 us (94%)
  other arithmetic  16.8 us (5%)
    pallas_call x1, Pallas kernels, gradients_of(): pl.pallas_call(functools.partial(kernel, n, float(n * (wg.size + wu.size...  342 us
    convert_element_type x2, other arithmetic, adamw(): return ((w - 0.02 * step).astype(BF16), m, v)  16.8 us

profile of v2, /device:TPU:113, one launch (start us, length us, event | category | flops | bytes accessed | tf_op | source)
XLA Modules:
  0.0 362.0 jit_solution(2823740041593118971)
XLA Ops:
  0.6 341.8 %shard_map.178 = (bf16[22,8,192,512]{3,2,1,0:T(8,128)(2,1)}, bf16[11,2048,256]{2,1,0:T(8,128)(2,1)}, f32[11,2048,512]{2,1,0:T(8,128)}, bf16[1024,2048]{1,0:T(8,1...) custom-call(bf16[2048,1024]{1,0:T(8,128)(2,1)} %bitcast.3, ...), custom_call_target="tpu_custom_call" | custom-call | flops 177167400960 | bytes 200000000 | tf_op jit(solution)/shard_map/pallas_call | solution.py:545
  342.5 1.2 slice.3
  343.7 0.0 copy-start
  343.7 0.0 copy-start.1
  343.7 0.0 copy-start.2
  343.7 0.0 copy-start.3
  343.7 0.0 copy-start.4
  343.7 0.0 copy-start.5
  343.8 0.0 copy-start.6
  343.8 9.2 %fusion.8 = (bf16[2,352,1024]{2,1,0:T(8,128)(2,1)}, f32[2,352,1024]{2,1,0:T(8,128)}, f32[2,352,1024]{2,1,0:T(8,128)}) fusion(bf16[2,352,1024]{2,1,0:T(8,128)(2,1)} %wd.1, f32[]{:T(128)} %bitcast.2, bf16[2,352,1024]{2,1,0:T(8,128)(2,1)} %get-tuple-element.16, f32[2,352,1024]{2,1,0:T(8,128)} %param.21, f32[2,352,1024]{2,1,0:T(8,128)} %param.18), kind=kLoop, calls=%fused_computation.17 | loop fusion | flops 12255232 | bytes 15859716 | tf_op jit(solution)/shard_map/convert_element_type | solution.py:613
  352.9 0.0 copy-done
  352.9 0.0 copy-done.1
  352.9 0.0 copy-done.2
  353.0 0.0 copy-done.3
  353.0 0.0 copy-done.4
  353.0 1.0 copy-done.5
  353.9 0.4 copy-done.6
  354.4 7.6 %fusion.2 = (bf16[2,128,2816]{2,1,0:T(8,128)(2,1)}, f32[2,128,2816]{2,1,0:T(8,128)}, f32[2,128,2816]{2,1,0:T(8,128)}, bf16[2,128,2816]{2,1,0:T(8,128)(2,1)}, f32...) fusion(bf16[2,128,2816]{2,1,0:T(8,128)(2,1)S(1)} %copy-done.4, f32[]{:T(128)} %bitcast.2, ...), kind=kLoop, calls=%fused_computation.11 | loop fusion | flops 24510464 | bytes 31719428 | tf_op jit(solution)/shard_map/convert_element_type | solution.py:613
Async XLA Ops:
  343.7 9.2 %copy-start = (f32[2,128,2816]{2,1,0:T(8,128)S(1)}, f32[2,128,2816]{2,1,0:T(8,128)}, u32[]{:S(2)}) copy-start(f32[2,128,2816]{2,1,0:T(8,128)} %param.19) | copy-start | bytes 8650756
  343.7 9.2 %copy-start.1 = (f32[2,128,2816]{2,1,0:T(8,128)S(1)}, f32[2,128,2816]{2,1,0:T(8,128)}, u32[]{:S(2)}) copy-start(f32[2,128,2816]{2,1,0:T(8,128)} %param.16) | copy-start | bytes 8650756
  343.7 9.2 %copy-start.2 = (f32[2,128,2816]{2,1,0:T(8,128)S(1)}, f32[2,128,2816]{2,1,0:T(8,128)}, u32[]{:S(2)}) copy-start(f32[2,128,2816]{2,1,0:T(8,128)} %param.20) | copy-start | bytes 8650756
  343.7 9.2 %copy-start.3 = (f32[2,128,2816]{2,1,0:T(8,128)S(1)}, f32[2,128,2816]{2,1,0:T(8,128)}, u32[]{:S(2)}) copy-start(f32[2,128,2816]{2,1,0:T(8,128)} %param.17) | copy-start | bytes 8650756
  343.7 9.2 %copy-start.4 = (bf16[2,128,2816]{2,1,0:T(8,128)(2,1)S(1)}, bf16[2,128,2816]{2,1,0:T(8,128)(2,1)}, u32[]{:S(2)}) copy-start(bf16[2,128,2816]{2,1,0:T(8,128)(2,1)} %wg.1) | copy-start | bytes 4325380
  343.7 10.2 %copy-start.5 = (bf16[2,128,2816]{2,1,0:T(8,128)(2,1)S(1)}, bf16[2,128,2816]{2,1,0:T(8,128)(2,1)}, u32[]{:S(2)}) copy-start(bf16[2,128,2816]{2,1,0:T(8,128)(2,1)} %wu.1) | copy-start | bytes 4325380
  343.8 10.6 %copy-start.6 = (bf16[2,128,2816]{2,1,0:T(8,128)(2,1)S(1)}, bf16[2,128,2816]{2,1,0:T(8,128)(2,1)}, u32[]{:S(2)}) copy-start(bf16[2,128,2816]{2,1,0:T(8,128)(2,1)} %get-tuple-element.13) | copy-start | bytes 4325380

commit v3 on v2

--- a/solution.py
+++ b/solution.py
@@ -272,7 +272,9 @@
             dst[q : q + 256, pl.ds(start, size)] = block[:, q : q + 256].T.astype(BF16)
 
     def gates(rows, b):
-        both = dot(va[rows, :], wgu_b[b].reshape(d, 2 * wide))
+        return gated(dot(va[rows, :], wgu_b[b].reshape(d, 2 * wide)))
+
+    def gated(both):
         g, u = both[:, :wide], both[:, wide:]
         sig = jax.nn.sigmoid(g)
         silu = g * sig
@@ -407,10 +409,6 @@
         def _():
             e2(t + 2)
 
-        @pl.when(t + 1 < chunks)
-        def _():
-            e3(t + 1)
-
         @pl.when(t + 4 < chunks)
         def _():
             e1(t + 4)
@@ -419,30 +417,46 @@
             copy.wait()
         b = lax.rem(t, 2)
 
-        def work(i, _):
-            rows = pl.ds(pl.multiple_of(i * BLOCK, BLOCK), BLOCK)
-            silu, slope, hidden = gates(rows, b)
-            by = dot_t(vc[rows, :], wd_b[b].reshape(n * ROWS, d)).astype(BF16).astype(F32)
+        def ahead(i):
+            rows = slice(i * BLOCK, (i + 1) * BLOCK)
+            both = dot(va[rows, :], wgu_b[b].reshape(d, 2 * wide))
+            return both, dot_t(vc[rows, :], wd_b[b].reshape(n * ROWS, d))
+
+        def behind(i, both, by):
+            rows = slice(i * BLOCK, (i + 1) * BLOCK)
+            silu, slope, hidden = gated(both)
+            by = by.astype(BF16).astype(F32)
             act[0, rows, :] = hidden
-            dg, du = (by * slope).astype(BF16), (by * silu).astype(BF16)
-            dgu[rows, 0:wide] = dg
-            dgu[rows, wide:] = du
-            acc[rows, :] += dot_t(jnp.concatenate([dg, du], axis=1), wgu_b[b].reshape(d, 2 * wide))
-            return 0
-
-        lax.fori_loop(0, blocks, work, 0)
+            dgu[rows, 0:wide] = (by * slope).astype(BF16)
+            dgu[rows, wide:] = (by * silu).astype(BF16)
+            acc[rows, :] += dot_t(dgu[rows, :], wgu_b[b].reshape(d, 2 * wide))
+
+        def work(start, stop):
+            held = ahead(start)
+            for i in range(start, stop):
+                later = ahead(i + 1) if i + 1 < stop else None
+                behind(i, *held)
+                held = later
+
+        work(0, blocks // 2)
+
+        @pl.when(r >= 4)
+        def _():
+            f4(r - 4)
+
+        @pl.when(r >= 1)
+        def _():
+            f2(r - 1)
 
         @pl.when(t + 1 < chunks)
         def _():
+            e3(t + 1)
+
+        work(blocks // 2, blocks)
+
+        @pl.when(t + 1 < chunks)
+        def _():
             e4(t + 1)
-
-        @pl.when(r >= 4)
-        def _():
-            f4(r - 4)
-
-        @pl.when(r >= 1)
-        def _():
-            f2(r - 1)
 
         @pl.when(r >= 2)
         def _():
@@ -486,14 +500,18 @@
             for copy in saved(s + 1):
                 copy.start()
 
-        def work(i, _):
-            rows = pl.ds(pl.multiple_of(i * BLOCK, BLOCK), BLOCK)
-            by = dot_t(vc[rows, :], wd_b[b].reshape(n * ROWS, d)).astype(BF16).astype(F32)
+        def ahead(i):
+            return dot_t(vc[i * BLOCK : (i + 1) * BLOCK, :], wd_b[b].reshape(n * ROWS, d))
+
+        held = ahead(0)
+        for i in range(blocks):
+            later = ahead(i + 1) if i + 1 < blocks else None
+            rows = slice(i * BLOCK, (i + 1) * BLOCK)
+            by = held.astype(BF16).astype(F32)
             dgu[rows, 0:wide] = (by * sgu[b, rows, 0:wide]).astype(BF16)
             dgu[rows, wide:] = (by * sgu[b, rows, wide:]).astype(BF16)
-            return 0
-
-        lax.fori_loop(0, blocks, work, 0)
+            held = later
+
         f4(r - 4)
         f2(r - 1)
         f3(r - 2)
@@ -529,7 +547,7 @@
     for copy in sends:
         copy.wait_send()
     total = jnp.sum(norms[...])
-    fac[...] = jnp.minimum(1.0, 0.5 * lax.rsqrt(jnp.full(fac.shape, total / count, F32) + 1e-30))
+    fac[...] = jnp.minimum(1.0, 0.5 * lax.rsqrt(jnp.full((8, 128), total / count, F32) + 1e-30))[0:1, 0:1]
 
 
 def gradients_of(n, x, dy, wg, wu, wd):
@@ -552,7 +570,7 @@
             jax.ShapeDtypeStruct(wg.shape, BF16),
             jax.ShapeDtypeStruct(wu.shape, BF16),
             jax.ShapeDtypeStruct(wd.shape, BF16),
-            jax.ShapeDtypeStruct((8, 128), F32),
+            jax.ShapeDtypeStruct((1, 1), F32),
         ),
         in_specs=[hbm, hbm, vmem, vmem, vmem],
         out_specs=(hbm, hbm, hbm, hbm, vmem, vmem, vmem, vmem),
@@ -603,7 +621,7 @@
             flops=30 * tokens * d * ff, bytes_accessed=200_000_000, transcendentals=2 * layers * tokens * ff
         ),
     )(x, dy, wg, wu, wd)
-    return out[4:7], out[7][0, 0]
+    return out[4:7], out[7].reshape(())
 
 
 def adamw(w, m, v, g):

time: 362 us -> 337 us (0.931)
  Pallas kernels: 342 us -> 317 us
    pallas_call x1, Pallas kernels: 342 us -> 317 us  [gradients_of(): pl.pallas_call(functools.partial(kernel, n, float(n * (wg.size + wu.size...]
where the time goes in v3:
time: 337 us; the launch traced here: 336 us
  Pallas kernels  317 us (94%)
  other arithmetic  17 us (5%)
    pallas_call x1, Pallas kernels, gradients_of(): pl.pallas_call(functools.partial(kernel, n, float(n * (wg.size + wu.size...  317 us
    convert_element_type x2, other arithmetic, adamw(): return ((w - 0.02 * step).astype(BF16), m, v)  17 us

profile of v3, /device:TPU:113, one launch (start us, length us, event | category | flops | bytes accessed | tf_op | source)
XLA Modules:
  0.0 336.4 jit_solution(14404459208530679895)
XLA Ops:
  0.6 317.4 %shard_map.178 = (bf16[22,8,192,512]{3,2,1,0:T(8,128)(2,1)}, bf16[11,2048,256]{2,1,0:T(8,128)(2,1)}, f32[11,2048,512]{2,1,0:T(8,128)}, bf16[1024,2048]{1,0:T(8,1...) custom-call(bf16[2048,1024]{1,0:T(8,128)(2,1)} %bitcast.3, ...), custom_call_target="tpu_custom_call" | custom-call | flops 177167400960 | bytes 200000000 | tf_op jit(solution)/shard_map/pallas_call | solution.py:563
  318.0 0.0 copy-start
  318.0 0.0 copy-start.1
  318.0 0.0 copy-start.2
  318.0 0.0 copy-start.3
  318.1 0.0 copy-start.4
  318.1 0.0 copy-start.5
  318.1 0.0 copy-start.6
  318.1 9.3 %fusion.8 = (bf16[2,352,1024]{2,1,0:T(8,128)(2,1)}, f32[2,352,1024]{2,1,0:T(8,128)}, f32[2,352,1024]{2,1,0:T(8,128)}) fusion(bf16[2,352,1024]{2,1,0:T(8,128)(2,1)} %wd.1, f32[]{:T(128)} %bitcast.2, bf16[2,352,1024]{2,1,0:T(8,128)(2,1)} %get-tuple-element.16, f32[2,352,1024]{2,1,0:T(8,128)} %param.21, f32[2,352,1024]{2,1,0:T(8,128)} %param.18), kind=kLoop, calls=%fused_computation.17 | loop fusion | flops 12255232 | bytes 15859716 | tf_op jit(solution)/shard_map/convert_element_type | solution.py:631
  327.4 0.0 copy-done
  327.4 0.0 copy-done.1
  327.4 0.0 copy-done.2
  327.4 0.0 copy-done.3
  327.4 0.0 copy-done.4
  327.4 0.6 copy-done.5
  328.0 0.6 copy-done.6
  328.7 7.7 %fusion.2 = (bf16[2,128,2816]{2,1,0:T(8,128)(2,1)}, f32[2,128,2816]{2,1,0:T(8,128)}, f32[2,128,2816]{2,1,0:T(8,128)}, bf16[2,128,2816]{2,1,0:T(8,128)(2,1)}, f32...) fusion(bf16[2,128,2816]{2,1,0:T(8,128)(2,1)S(1)} %copy-done.4, f32[]{:T(128)} %bitcast.2, ...), kind=kLoop, calls=%fused_computation.11 | loop fusion | flops 24510464 | bytes 31719428 | tf_op jit(solution)/shard_map/convert_element_type | solution.py:631
Async XLA Ops:
  318.0 9.4 %copy-start = (f32[2,128,2816]{2,1,0:T(8,128)S(1)}, f32[2,128,2816]{2,1,0:T(8,128)}, u32[]{:S(2)}) copy-start(f32[2,128,2816]{2,1,0:T(8,128)} %param.19) | copy-start | bytes 8650756
  318.0 9.4 %copy-start.1 = (f32[2,128,2816]{2,1,0:T(8,128)S(1)}, f32[2,128,2816]{2,1,0:T(8,128)}, u32[]{:S(2)}) copy-start(f32[2,128,2816]{2,1,0:T(8,128)} %param.16) | copy-start | bytes 8650756
  318.0 9.3 %copy-start.2 = (f32[2,128,2816]{2,1,0:T(8,128)S(1)}, f32[2,128,2816]{2,1,0:T(8,128)}, u32[]{:S(2)}) copy-start(f32[2,128,2816]{2,1,0:T(8,128)} %param.20) | copy-start | bytes 8650756
  318.0 9.3 %copy-start.3 = (f32[2,128,2816]{2,1,0:T(8,128)S(1)}, f32[2,128,2816]{2,1,0:T(8,128)}, u32[]{:S(2)}) copy-start(f32[2,128,2816]{2,1,0:T(8,128)} %param.17) | copy-start | bytes 8650756
  318.1 9.3 %copy-start.4 = (bf16[2,128,2816]{2,1,0:T(8,128)(2,1)S(1)}, bf16[2,128,2816]{2,1,0:T(8,128)(2,1)}, u32[]{:S(2)}) copy-start(bf16[2,128,2816]{2,1,0:T(8,128)(2,1)} %wg.1) | copy-start | bytes 4325380
  318.1 10.0 %copy-start.5 = (bf16[2,128,2816]{2,1,0:T(8,128)(2,1)S(1)}, bf16[2,128,2816]{2,1,0:T(8,128)(2,1)}, u32[]{:S(2)}) copy-start(bf16[2,128,2816]{2,1,0:T(8,128)(2,1)} %wu.1) | copy-start | bytes 4325380
  318.1 10.6 %copy-start.6 = (bf16[2,128,2816]{2,1,0:T(8,128)(2,1)S(1)}, bf16[2,128,2816]{2,1,0:T(8,128)(2,1)}, u32[]{:S(2)}) copy-start(bf16[2,128,2816]{2,1,0:T(8,128)(2,1)} %get-tuple-element.13) | copy-start | bytes 4325380

commit v4 on v3

--- a/solution.py
+++ b/solution.py
@@ -26,7 +26,7 @@
     n, count,
     x, dy, wg, wu, wd,
     gath, act_st, sgu_st, a0t_st, gg, gu, gd, fac,
-    va, vat, vc, vct, acc, act, sgu, dgu, wgu_b, wd_b,
+    va, vat, vc, vct, acc, act, sgu, dgu, rest, wgu_b, wd_b,
     own, term, pair, part, fin, halves, wholes, squares, norms,
     in_sem, own_send, own_local, full_recv, half_recv, part_recv, fwd_send, load_sem, stash_sem, saved_sem,
     pair_send, pair_recv, b_send, b_recv, c_send, c_recv, norm_send, norm_recv,
@@ -269,7 +269,7 @@
 
     def turn(block, dst, start, size):
         for q in range(0, d, 256):
-            dst[q : q + 256, pl.ds(start, size)] = block[:, q : q + 256].T.astype(BF16)
+            dst[q : q + 256, pl.ds(start, size)] = block[:, q : q + 256].T
 
     def gates(rows, b):
         return gated(dot(va[rows, :], wgu_b[b].reshape(d, 2 * wide)))
@@ -326,7 +326,7 @@
         h = va[rows, :].astype(F32)
         a = (h * lax.rsqrt(jnp.mean(h * h, -1, keepdims=True) + 1e-6)).astype(BF16)
         va[rows, :] = a
-        turn(a.astype(F32), vat, start, 256)
+        turn(a, vat, start, 256)
         acc[rows, :] = jnp.zeros((256, d), F32)
         return 0
 
@@ -339,7 +339,7 @@
 
     def second(i, _):
         start = pl.multiple_of(i * 256, 256)
-        turn(vc[pl.ds(start, 256), :].astype(F32), vct, start, 256)
+        turn(vc[pl.ds(start, 256), :], vct, start, 256)
         return 0
 
     lax.fori_loop(0, tokens // 256, second, 0)
@@ -351,6 +351,11 @@
     gu[...] = jnp.zeros_like(gu)
     squares[...] = jnp.zeros_like(squares)
 
+    half = tokens // 2
+    x_again = [
+        pltpu.make_async_copy(x.at[i * half : (i + 1) * half], va.at[i * half : (i + 1) * half], in_sem.at[i]) for i in range(2)
+    ]
+
     def forward(t, _):
         e2(t + 2)
         e3(t + 1)
@@ -375,32 +380,42 @@
 
         lax.fori_loop(0, blocks // 2, work, 0)
         e4(t + 1)
+
+        @pl.when(t == slots - 1)
+        def _():
+            x_again[0].start()
+
         lax.fori_loop(blocks // 2, blocks, work, 0)
         for copy in stashes(t, b):
             copy.start()
         return 0
 
     lax.fori_loop(0, slots, forward, 0)
-    x_in.start()
+    x_again[1].start()
     a0t_out.wait()
-    for t in (slots - 2, slots - 1):
-        for copy in stashes(t, t % 2):
-            copy.wait()
-    x_in.wait()
+    last = (slots - 1) % 2
+    for copy in stashes(slots - 2, 1 - last):
+        copy.wait()
+    x_again[0].wait()
 
     def between(i, _):
         start = pl.multiple_of(i * 256, 256)
         rows = pl.ds(start, 256)
         h = (va[rows, :].astype(F32) + acc[rows, :].astype(BF16).astype(F32)).astype(BF16).astype(F32)
-        sgu[0, rows, :] = h[:, : 2 * wide]
-        sgu[1, rows, :] = h[:, 2 * wide :]
+        sgu[1 - last, rows, :] = h[:, : 2 * wide]
+        act[1 - last, rows, :] = h[:, 2 * wide : 3 * wide].astype(BF16)
+        rest[rows, :] = h[:, 3 * wide :].astype(BF16)
         a = (h * lax.rsqrt(jnp.mean(h * h, -1, keepdims=True) + 1e-6)).astype(BF16)
         va[rows, :] = a
-        turn(a.astype(F32), vat, start, 256)
+        turn(a, vat, start, 256)
         acc[rows, :] = jnp.zeros((256, d), F32)
         return 0
 
-    lax.fori_loop(0, tokens // 256, between, 0)
+    lax.fori_loop(0, half // 256, between, 0)
+    x_again[1].wait()
+    lax.fori_loop(half // 256, tokens // 256, between, 0)
+    for copy in stashes(slots - 1, last):
+        copy.wait()
 
     def both_ways(t, _):
         r = t - slots
@@ -426,7 +441,7 @@
             rows = slice(i * BLOCK, (i + 1) * BLOCK)
             silu, slope, hidden = gated(both)
             by = by.astype(BF16).astype(F32)
-            act[0, rows, :] = hidden
+            act[last, rows, :] = hidden
             dgu[rows, 0:wide] = (by * slope).astype(BF16)
             dgu[rows, wide:] = (by * silu).astype(BF16)
             acc[rows, :] += dot_t(dgu[rows, :], wgu_b[b].reshape(d, 2 * wide))
@@ -462,31 +477,30 @@
         def _():
             f3(r - 2)
 
-        gradients(r, 0)
+        gradients(r, last)
         f1(r)
         return 0
 
     lax.fori_loop(slots, chunks, both_ways, 0)
     a0t_in = pltpu.make_async_copy(a0t_st, vat, in_sem.at[2])
     a0t_in.start()
-    for copy in saved(0)[:3]:
+    for copy in saved(0):
         copy.start()
 
     def back(i, _):
         start = pl.multiple_of(i * 256, 256)
         rows = pl.ds(start, 256)
-        h = jnp.concatenate([sgu[0, rows, :], sgu[1, rows, :]], axis=1)
+        h = jnp.concatenate([sgu[1 - last, rows, :], act[1 - last, rows, :].astype(F32), rest[rows, :].astype(F32)], axis=1)
         da = acc[rows, :].astype(BF16).astype(F32)
         scale = lax.rsqrt(jnp.mean(h * h, -1, keepdims=True) + 1e-6)
         along = jnp.mean(da * h, -1, keepdims=True)
         by_h = (da * scale - h * (scale * scale * scale * along)).astype(BF16).astype(F32)
         by_h = (vc[rows, :].astype(F32) + by_h).astype(BF16)
         vc[rows, :] = by_h
-        turn(by_h.astype(F32), vct, start, 256)
+        turn(by_h, vct, start, 256)
         return 0
 
     lax.fori_loop(0, tokens // 256, back, 0)
-    saved(0)[3].start()
     a0t_in.wait()
 
     def backward(t, _):
@@ -583,6 +597,7 @@
             pltpu.VMEM((2, tokens, wide), BF16),
             pltpu.VMEM((2, tokens, 2 * wide), F32),
             pltpu.VMEM((tokens, 2 * wide), BF16),
+            pltpu.VMEM((tokens, wide), BF16),
             pltpu.VMEM((2, n, tall, 2 * wide), BF16),
             pltpu.VMEM((2, n, ROWS, d), BF16),
             pltpu.VMEM((OWN, high, 2 * wide), BF16),

time: 337 us -> 332 us (0.985)
  Pallas kernels: 317 us -> 312 us
    pallas_call x1, Pallas kernels: 317 us -> 312 us  [gradients_of(): pl.pallas_call(functools.partial(kernel, n, float(n * (wg.size + wu.size...]
where the time goes in v4:
time: 332 us; the launch traced here: 331 us
  Pallas kernels  312 us (94%)
  other arithmetic  17 us (5%)
    pallas_call x1, Pallas kernels, gradients_of(): pl.pallas_call(functools.partial(kernel, n, float(n * (wg.size + wu.size...  312 us
    convert_element_type x2, other arithmetic, adamw(): return ((w - 0.02 * step).astype(BF16), m, v)  17 us

profile of v4, /device:TPU:113, one launch (start us, length us, event | category | flops | bytes accessed | tf_op | source)
XLA Modules:
  0.0 331.3 jit_solution(16141694819975343979)
XLA Ops:
  0.6 312.3 %shard_map.178 = (bf16[22,8,192,512]{3,2,1,0:T(8,128)(2,1)}, bf16[11,2048,256]{2,1,0:T(8,128)(2,1)}, f32[11,2048,512]{2,1,0:T(8,128)}, bf16[1024,2048]{1,0:T(8,1...) custom-call(bf16[2048,1024]{1,0:T(8,128)(2,1)} %bitcast.3, ...), custom_call_target="tpu_custom_call" | custom-call | flops 177167400960 | bytes 200000000 | tf_op jit(solution)/shard_map/pallas_call | solution.py:577
  313.0 0.0 copy-start
  313.0 0.0 copy-start.1
  313.0 0.0 copy-start.2
  313.0 0.0 copy-start.3
  313.0 0.0 copy-start.4
  313.0 0.0 copy-start.5
  313.1 0.0 copy-start.6
  313.1 9.3 %fusion.8 = (bf16[2,352,1024]{2,1,0:T(8,128)(2,1)}, f32[2,352,1024]{2,1,0:T(8,128)}, f32[2,352,1024]{2,1,0:T(8,128)}) fusion(bf16[2,352,1024]{2,1,0:T(8,128)(2,1)} %wd.1, f32[]{:T(128)} %bitcast.2, bf16[2,352,1024]{2,1,0:T(8,128)(2,1)} %get-tuple-element.16, f32[2,352,1024]{2,1,0:T(8,128)} %param.21, f32[2,352,1024]{2,1,0:T(8,128)} %param.18), kind=kLoop, calls=%fused_computation.17 | loop fusion | flops 12255232 | bytes 15859716 | tf_op jit(solution)/shard_map/convert_element_type | solution.py:646
  322.3 0.0 copy-done
  322.3 0.0 copy-done.1
  322.3 0.0 copy-done.2
  322.3 0.0 copy-done.3
  322.4 0.0 copy-done.4
  322.4 0.6 copy-done.5
  323.0 0.6 copy-done.6
  323.6 7.7 %fusion.2 = (bf16[2,128,2816]{2,1,0:T(8,128)(2,1)}, f32[2,128,2816]{2,1,0:T(8,128)}, f32[2,128,2816]{2,1,0:T(8,128)}, bf16[2,128,2816]{2,1,0:T(8,128)(2,1)}, f32...) fusion(bf16[2,128,2816]{2,1,0:T(8,128)(2,1)S(1)} %copy-done.4, f32[]{:T(128)} %bitcast.2, ...), kind=kLoop, calls=%fused_computation.11 | loop fusion | flops 24510464 | bytes 31719428 | tf_op jit(solution)/shard_map/convert_element_type | solution.py:646
Async XLA Ops:
  313.0 9.4 %copy-start = (f32[2,128,2816]{2,1,0:T(8,128)S(1)}, f32[2,128,2816]{2,1,0:T(8,128)}, u32[]{:S(2)}) copy-start(f32[2,128,2816]{2,1,0:T(8,128)} %param.19) | copy-start | bytes 8650756
  313.0 9.4 %copy-start.1 = (f32[2,128,2816]{2,1,0:T(8,128)S(1)}, f32[2,128,2816]{2,1,0:T(8,128)}, u32[]{:S(2)}) copy-start(f32[2,128,2816]{2,1,0:T(8,128)} %param.16) | copy-start | bytes 8650756
  313.0 9.3 %copy-start.2 = (f32[2,128,2816]{2,1,0:T(8,128)S(1)}, f32[2,128,2816]{2,1,0:T(8,128)}, u32[]{:S(2)}) copy-start(f32[2,128,2816]{2,1,0:T(8,128)} %param.20) | copy-start | bytes 8650756
  313.0 9.3 %copy-start.3 = (f32[2,128,2816]{2,1,0:T(8,128)S(1)}, f32[2,128,2816]{2,1,0:T(8,128)}, u32[]{:S(2)}) copy-start(f32[2,128,2816]{2,1,0:T(8,128)} %param.17) | copy-start | bytes 8650756
  313.0 9.3 %copy-start.4 = (bf16[2,128,2816]{2,1,0:T(8,128)(2,1)S(1)}, bf16[2,128,2816]{2,1,0:T(8,128)(2,1)}, u32[]{:S(2)}) copy-start(bf16[2,128,2816]{2,1,0:T(8,128)(2,1)} %wg.1) | copy-start | bytes 4325380
  313.0 10.0 %copy-start.5 = (bf16[2,128,2816]{2,1,0:T(8,128)(2,1)S(1)}, bf16[2,128,2816]{2,1,0:T(8,128)(2,1)}, u32[]{:S(2)}) copy-start(bf16[2,128,2816]{2,1,0:T(8,128)(2,1)} %wu.1) | copy-start | bytes 4325380
  313.1 10.6 %copy-start.6 = (bf16[2,128,2816]{2,1,0:T(8,128)(2,1)S(1)}, bf16[2,128,2816]{2,1,0:T(8,128)(2,1)}, u32[]{:S(2)}) copy-start(bf16[2,128,2816]{2,1,0:T(8,128)(2,1)} %get-tuple-element.13) | copy-start | bytes 4325380
